TPU v7x, 256 devices: a whole 4x4x8 slice. The times are simulated.
256 devices in a mesh: row: 8 (over y, z_lo), col: 4 (over z_hi), depth: 8 (over x, core).
Axes of the slice: x: 4, y: 4, z: 8 (z_hi: 4, z_lo: 2; z = z_hi * 2 + z_lo), core: 2. Of those that a mesh axis runs over, the one named last changes fastest.
Arguments:
- grad_out: bfloat16 [2048, 6144], P('depth', 'col'), may hold values from -6 to 6
- pre_act: bfloat16 [2048, 24576], P('depth', 'row'), may hold values from -8 to 8
- down_weight: bfloat16 [24576, 6144], P(('row', 'depth'), 'col'), may hold values from -0.109375 to 0.109375
Outputs:
- grad_pre: bfloat16 [2048, 24576], P('depth', 'row')
- grad_weight: bfloat16 [24576, 6144], P(('row', 'depth'), 'col')
All inputs are finite; a program needn't handle non-finite values.
Results may differ from a plain program's by a relative error of at most 0.0066.
Values may be sent and summed in bfloat16 or wider, within the bound.
A program may use at most 64 MiB of HBM per device.

v0:
```python
import jax
import jax.numpy as jnp
from jax import lax
from jax.sharding import PartitionSpec as P

sqrt_two_pi = 0.7978845608028654
cubic_coeff = 0.044715


def split_up(array, dim, count):
    dims = array.shape
    pieces = array.reshape(*dims[:dim], count, dims[dim] // count, *dims[dim + 1 :])
    return jnp.moveaxis(pieces, dim, 0)


def sum_at_owner(array, axis, dim):
    count = lax.axis_size(axis)
    pieces = lax.all_to_all(split_up(array, dim, count), axis, 0, 0, tiled=True)
    return jnp.sum(pieces.astype(jnp.float32), axis=0)


def sent_to_all(array, axis):
    count = lax.axis_size(axis)
    return lax.all_to_all(
        jnp.broadcast_to(array[None], (count, *array.shape)), axis, 0, 0, tiled=True
    )


def laid_out(pieces, dim):
    dims = list(pieces.shape[1:])
    dims[dim] *= pieces.shape[0]
    return jnp.moveaxis(pieces, 0, dim).reshape(dims)


def collect(array, axis, dim):
    pieces = sent_to_all(array, axis)
    return laid_out(pieces, dim)


def gelu_value(preact):
    tangent = jnp.tanh(sqrt_two_pi * (preact + cubic_coeff * preact * preact * preact))
    return 0.5 * preact * (1.0 + tangent)


def gelu_slope(preact):
    tangent = jnp.tanh(sqrt_two_pi * (preact + cubic_coeff * preact * preact * preact))
    inner = sqrt_two_pi * (1.0 + 3.0 * cubic_coeff * preact * preact)
    return 0.5 * (1.0 + tangent) + 0.5 * preact * (1.0 - tangent * tangent) * inner


def contract_last(left, right):
    return lax.dot_general(
        left, right, (((1,), (1,)), ((), ())), preferred_element_type=jnp.float32
    )


def contract_first(left, right):
    return lax.dot_general(
        left, right, (((0,), (0,)), ((), ())), preferred_element_type=jnp.float32
    )


def finish_rows(partial_value, preacts):
    share = sum_at_owner(partial_value.astype(jnp.bfloat16), "col", 0)
    height = share.shape[0]
    offset = lax.axis_index("col") * height
    pre_rows = lax.dynamic_slice_in_dim(preacts, offset, height, 0)
    pieces = (share * gelu_slope(pre_rows.astype(jnp.float32))).astype(jnp.bfloat16)
    return collect(pieces, "col", 0)


def on_device(grad_out, pre_act, down_weight):
    every_grad = lax.all_gather(grad_out, "depth", axis=0, tiled=True)
    own_pre = lax.all_to_all(pre_act, "depth", split_axis=1, concat_axis=0, tiled=True)
    partial_value = contract_last(every_grad, down_weight)
    local_grad = finish_rows(partial_value, own_pre)
    grad_pre = lax.all_to_all(local_grad, "depth", split_axis=0, concat_axis=1, tiled=True)
    own_act = gelu_value(own_pre.astype(jnp.float32)).astype(jnp.bfloat16)
    grad_weight = contract_first(own_act, every_grad).astype(jnp.bfloat16)
    return (grad_pre, grad_weight)


def solution(mesh):
    placed = (P("depth", "col"), P("depth", "row"), P(("row", "depth"), "col"))
    return jax.shard_map(
        on_device,
        mesh=mesh,
        in_specs=placed,
        out_specs=(P("depth", "row"), P(("row", "depth"), "col")),
        check_vma=False,
    )
```

profile of v0, /device:TPU:56, one launch (start us, length us, event | category | flops | bytes accessed | tf_op | source)
XLA Modules:
  0.0 198.6 jit_solution(504990352886837358)
XLA Ops:
  7.2 0.0 copy-start
  7.2 0.0 all-gather.2.cloned.1.call-start
  7.2 0.7 all-gather.2.cloned.1.call-update
  7.9 2.6 %copy.5 = bf16[256,3072]{0,1:T(8,128)(2,1)} copy(bf16[256,3072]{1,0:T(8,128)(2,1)} %param.4) | data formatting | bytes 3145728 | tf_op args[1]
  10.5 4.3 %all-to-all-start.1 = ((bf16[256,8,384]{0,2,1:T(8,128)(2,1)}), bf16[256,8,384]{0,2,1:T(8,128)(2,1)S(1)}, u32[]{:S(2)}, u32[]{:S(2)}) async-start(bf16[256,8,384]{0,2,1:T(8,128)(2,1)} %bitcast.12), calls=%async_computation.1 | async-start | bytes 3145728 | tf_op jit(solution)/shard_map/all_to_all | solution.py:74
  14.8 48.3 %all-gather.2.cloned.1.call-done = bf16[2048,1536]{1,0:T(8,128)(2,1)} async-done(((bf16[256,1536]{1,0:T(8,128)(2,1)}), bf16[2048,1536]{1,0:T(8,128)(2,1)}) %all-gather.2.cloned.1.call-update) | async-done | bytes 6291472 | tf_op jit(solution)/shard_map/all_gather | solution.py:73
  63.0 0.0 copy-done
  63.0 7.4 %convolution_convert_fusion.1 = bf16[2048,384]{1,0:T(8,128)(2,1)} fusion(bf16[2048,1536]{1,0:T(8,128)(2,1)} %all-gather.2.cloned.1.call-done, bf16[384,1536]{1,0:T(8,128)(2,1)S(1)} %copy-done), kind=kOutput, calls=%fused_computation.12 | convolution fusion | flops 2416705536 | bytes 9043968 | tf_op jit(solution)/shard_map/dot_general | solution.py:52
  70.4 0.0 all-to-all-done.1
  70.4 7.6 %all-to-all-start = ((bf16[4,512,384]{2,1,0:T(8,128)(2,1)}), bf16[4,512,384]{2,1,0:T(8,128)(2,1)}, u32[]{:S(2)}, u32[]{:S(2)}) async-start(bf16[4,512,384]{2,1,0:T(8,128)(2,1)} %bitcast.17), calls=%async_computation | async-start | bytes 3145728 | tf_op jit(solution)/shard_map/all_to_all | solution.py:18
  78.0 1.6 copy.6
  79.5 38.5 %all-to-all-done = bf16[4,512,384]{2,1,0:T(8,128)(2,1)} async-done(((bf16[4,512,384]{2,1,0:T(8,128)(2,1)}), bf16[4,512,384]{2,1,0:T(8,128)(2,1)}, u32[]{:S(2)}, u32[]{:S(2)}) %all-to-all-start) | async-done | bytes 1572896 | tf_op jit(solution)/shard_map/all_to_all | solution.py:18
  118.0 1.7 convert_reduce_fusion
  119.8 1.5 fusion.16
  121.3 0.1 broadcast_in_dim.2
  121.4 41.0 %all_to_all.48 = bf16[4,512,384]{2,1,0:T(8,128)(2,1)} all-to-all(bf16[4,512,384]{2,1,0:T(8,128)(2,1)S(1)} %broadcast_in_dim.2), channel_id=1, replica_groups=mesh['row'=8,'col'=4,'depth'=8] {'col'}, dimensions={0} | all-to-all | bytes 3145728 | tf_op jit(solution)/shard_map/all_to_all | solution.py:24
  162.5 3.6 %all-to-all-start.3 = ((bf16[8,256,384]{2,1,0:T(8,128)(2,1)}), bf16[8,256,384]{2,1,0:T(8,128)(2,1)S(1)}, u32[]{:S(2)}, u32[]{:S(2)}) async-start(bf16[8,256,384]{2,1,0:T(8,128)(2,1)} %bitcast.13), calls=%async_computation.3 | async-start | bytes 3145728 | tf_op jit(solution)/shard_map/all_to_all | solution.py:77
  166.1 7.0 %convolution_convert_fusion = bf16[384,1536]{1,0:T(8,128)(2,1)} fusion(bf16[2048,1536]{1,0:T(8,128)(2,1)} %all-gather.2.cloned.1.call-done, bf16[2048,384]{1,0:T(8,128)(2,1)} %bitcast.16), kind=kOutput, calls=%fused_computation.11 | convolution fusion | flops 2424373248 | bytes 9043968 | tf_op jit(solution)/shard_map/dot_general | solution.py:58
  173.0 14.5 %all-to-all-done.3 = bf16[8,256,384]{2,1,0:T(8,128)(2,1)S(1)} async-done(((bf16[8,256,384]{2,1,0:T(8,128)(2,1)}), bf16[8,256,384]{2,1,0:T(8,128)(2,1)S(1)}, u32[]{:S(2)}, u32[]{:S(2)}) %all-to-all-start.3) | async-done | bytes 1572896 | tf_op jit(solution)/shard_map/all_to_all | solution.py:77
  187.5 1.6 copy.7
  189.2 2.6 %copy.8 = bf16[256,3072]{1,0:T(8,128)(2,1)} copy(bf16[256,3072]{0,1:T(8,128)(2,1)} %bitcast.14) | data formatting | bytes 3145728
Async XLA Ops:
  7.2 55.9 %copy-start = (bf16[384,1536]{1,0:T(8,128)(2,1)S(1)}, bf16[384,1536]{1,0:T(8,128)(2,1)}, u32[]{:S(2)}) copy-start(bf16[384,1536]{1,0:T(8,128)(2,1)} %param.5) | copy-start | bytes 3538948
  7.2 55.9 %all-gather.2.cloned.1.call-start = ((), (), s32[]{:S(2)}) async-start(), calls=%async_computation.4 | async-start | bytes 7077888 | tf_op jit(solution)/shard_map/all_gather | solution.py:73
  10.5 59.9 %all-to-all-start.1 = ((bf16[256,8,384]{0,2,1:T(8,128)(2,1)}), bf16[256,8,384]{0,2,1:T(8,128)(2,1)S(1)}, u32[]{:S(2)}, u32[]{:S(2)}) async-start(bf16[256,8,384]{0,2,1:T(8,128)(2,1)} %bitcast.12), calls=%async_computation.1 | async-start | bytes 3145728 | tf_op jit(solution)/shard_map/all_to_all | solution.py:74
  70.4 47.6 %all-to-all-start = ((bf16[4,512,384]{2,1,0:T(8,128)(2,1)}), bf16[4,512,384]{2,1,0:T(8,128)(2,1)}, u32[]{:S(2)}, u32[]{:S(2)}) async-start(bf16[4,512,384]{2,1,0:T(8,128)(2,1)} %bitcast.17), calls=%async_computation | async-start | bytes 3145728 | tf_op jit(solution)/shard_map/all_to_all | solution.py:18
  162.5 25.1 %all-to-all-start.3 = ((bf16[8,256,384]{2,1,0:T(8,128)(2,1)}), bf16[8,256,384]{2,1,0:T(8,128)(2,1)S(1)}, u32[]{:S(2)}, u32[]{:S(2)}) async-start(bf16[8,256,384]{2,1,0:T(8,128)(2,1)} %bitcast.13), calls=%async_computation.3 | async-start | bytes 3145728 | tf_op jit(solution)/shard_map/all_to_all | solution.py:77
Sparse Core Ops, SparseCore 0:
  9.8 53.1 all-gather.1
where the time goes:
time: 199 us
  waiting for transfers between devices  102 us (51%)
  blocking collectives  41 us (21%)
  starting transfers between devices  15.5 us (8%)
  matrix products  14.4 us (7%)
  between operations  14.1 us (7%)
  local copies, waits for them, and re-layouts  8.49 us (4%)
  other arithmetic  3.26 us (2%)
    all_gather x1, waiting for transfers between devices, on_device(): every_grad = lax.all_gather(grad_out, 'depth', axis=0, tiled=True)  48.3 us
    all_to_all x1, blocking collectives, sent_to_all(): lax.all_to_all(jnp.broadcast_to(array[None], (count, *array.shape)), axis...  41 us
    all_to_all x1, waiting for transfers between devices, sum_at_owner(): pieces = lax.all_to_all(split_up(array, dim, count), axis, 0, 0, tiled=True)  38.5 us
    all_to_all x1, waiting for transfers between devices, on_device(): lax.all_to_all(local_grad, 'depth', split_axis=0, concat_axis=1, tiled=True)  14.5 us
    all_to_all x1, starting transfers between devices, sum_at_owner(): pieces = lax.all_to_all(split_up(array, dim, count), axis, 0, 0, tiled=True)  7.55 us
    dot_general x1, matrix products, contract_last(): lax.dot_general(left, right, (((1,), (1,)), ((), ())), preferred_element_...  7.39 us
    dot_general x1, matrix products, contract_first(): lax.dot_general(left, right, (((0,), (0,)), ((), ())), preferred_element_...  6.99 us
    unnamed x4, local copies, waits for them, and re-layouts  5.16 us
  transfers between devices with their start and end apart: 4, of which 3 were waited for; matrix products, arithmetic and copies ran while one was open for 9% of the time, Pallas kernels for 0%

commit v1 on v0

--- a/solution.py
+++ b/solution.py
@@ -1,3 +1,4 @@
+import functools
 import jax
 import jax.numpy as jnp
 from jax import lax
@@ -5,6 +6,34 @@
 
 sqrt_two_pi = 0.7978845608028654
 cubic_coeff = 0.044715
+
+
+def _begin_strips_all(t0, array_dim):
+    heard = jax.lax.axis_size("depth")
+    kept_arr = jax.lax.axis_index("depth")
+    step_out, v1, local_out = (heard, kept_arr, t0.shape[array_dim])
+    chunks = tuple(((idx, (idx + 1) % step_out) for idx in range(step_out)))
+    last = jnp.zeros(
+        (*t0.shape[:array_dim], step_out * local_out, *t0.shape[array_dim + 1 :]), t0.dtype
+    )
+    last = lax.dynamic_update_slice_in_dim(last, t0, v1 * local_out, axis=array_dim)
+    res = carry_out = t0
+    r2 = step_out // 2
+    steps_seen = tuple(((idx, (idx - 1) % step_out) for idx in range(step_out)))
+    for ii in [*range(1, r2 + 1)]:
+        res = jax.lax.ppermute(res, "depth", chunks)
+        last = lax.dynamic_update_slice_in_dim(
+            last, res, (v1 - ii) % step_out * local_out, axis=array_dim
+        )
+        if ii < step_out - r2:
+            carry_out = jax.lax.ppermute(carry_out, "depth", steps_seen)
+            last = lax.dynamic_update_slice_in_dim(
+                last, carry_out, (v1 + ii) % step_out * local_out, axis=array_dim
+            )
+    return last
+
+
+fill_desk = functools.partial(_begin_strips_all, array_dim=0)
 
 
 def split_up(array, dim, count):
@@ -70,7 +99,7 @@
 
 
 def on_device(grad_out, pre_act, down_weight):
-    every_grad = lax.all_gather(grad_out, "depth", axis=0, tiled=True)
+    every_grad = fill_desk(grad_out)
     own_pre = lax.all_to_all(pre_act, "depth", split_axis=1, concat_axis=0, tiled=True)
     partial_value = contract_last(every_grad, down_weight)
     local_grad = finish_rows(partial_value, own_pre)

time: 199 us -> 191 us (0.960)
  between operations: 14.1 us -> 0.74 us
  starting transfers between devices: 15.5 us -> 27.3 us
  waiting for transfers between devices: 102 us -> 92.9 us
  local copies, waits for them, and re-layouts: 8.49 us -> 16.3 us
  matrix products: 14.4 us -> 11.5 us
  blocking collectives: 41 us -> 38.3 us
    all_gather x1 -> x0, waiting for transfers between devices: 48.3 us -> none  [on_device(): every_grad = lax.all_gather(grad_out, 'depth', axis=0, tiled=True)]
    ppermute x0 -> x7, waiting for transfers between devices: none -> 42.7 us  [the longest x4 28.1 us: _begin_strips_all(): res = jax.lax.ppermute(res, 'depth', chunks)]
    ppermute x0 -> x7, starting transfers between devices: none -> 8.98 us  [the longest x3 8.96 us: _begin_strips_all(): carry_out = jax.lax.ppermute(carry_out, 'depth', steps_seen)]
    dynamic_update_slice x0 -> x8, local copies, waits for them, and re-layouts: none -> 3.86 us  [the longest x3 2.44 us: _begin_strips_all(): lax.dynamic_update_slice_in_dim(last, carry_out, (v1 + ii) % step_out * l...]
    unnamed x4 -> x12, local copies, waits for them, and re-layouts: 5.16 us -> 8.69 us
    all_to_all x1, starting transfers between devices: 3.58 us -> 6.52 us  [on_device(): lax.all_to_all(local_grad, 'depth', split_axis=0, concat_axis=1, tiled=True)]
    dot_general x1, matrix products: 7.39 us -> 4.5 us  [contract_last(): lax.dot_general(left, right, (((1,), (1,)), ((), ())), preferred_element_...]
    all_to_all x1, waiting for transfers between devices: 38.5 us -> 35.6 us  [sum_at_owner(): pieces = lax.all_to_all(split_up(array, dim, count), axis, 0, 0, tiled=True)]
  transfers between devices with their start and end apart: 4 -> 10, of which waited for: 3 -> 7; matrix products, arithmetic and copies ran while one was open for 9% -> 10% of each run, Pallas kernels for 0% -> 0%
where the time goes in v1:
time: 191 us; the launch traced here: 190 us
  waiting for transfers between devices  92.9 us (49%)
  blocking collectives  38.3 us (20%)
  starting transfers between devices  27.3 us (14%)
  local copies, waits for them, and re-layouts  16.3 us (9%)
  matrix products  11.5 us (6%)
  other arithmetic  3.24 us (2%)
    all_to_all x1, blocking collectives, sent_to_all(): lax.all_to_all(jnp.broadcast_to(array[None], (count, *array.shape)), axis...  38.3 us
    all_to_all x1, waiting for transfers between devices, sum_at_owner(): pieces = lax.all_to_all(split_up(array, dim, count), axis, 0, 0, tiled=True)  35.6 us
    ppermute x4, waiting for transfers between devices, _begin_strips_all(): res = jax.lax.ppermute(res, 'depth', chunks)  28.1 us
    ppermute x3, waiting for transfers between devices, _begin_strips_all(): carry_out = jax.lax.ppermute(carry_out, 'depth', steps_seen)  14.7 us
    all_to_all x1, waiting for transfers between devices, on_device(): lax.all_to_all(local_grad, 'depth', split_axis=0, concat_axis=1, tiled=True)  14.6 us
    ppermute x3, starting transfers between devices, _begin_strips_all(): carry_out = jax.lax.ppermute(carry_out, 'depth', steps_seen)  8.96 us
    unnamed x12, local copies, waits for them, and re-layouts  8.69 us
    all_to_all x1, starting transfers between devices, sum_at_owner(): pieces = lax.all_to_all(split_up(array, dim, count), axis, 0, 0, tiled=True)  7.56 us
  transfers between devices with their start and end apart: 10, of which 7 were waited for; matrix products, arithmetic and copies ran while one was open for 10% of the time, Pallas kernels for 0%

profile of v1, /device:TPU:56, one launch (start us, length us, event | category | flops | bytes accessed | tf_op | source)
XLA Modules:
  0.0 190.3 jit_solution(15819615060621878168)
XLA Ops:
  0.6 0.0 copy-start
  0.6 0.0 collective-permute-start
  0.7 2.9 %collective-permute-start.1 = (bf16[256,1536]{1,0:T(8,128)(2,1)}, bf16[256,1536]{1,0:T(8,128)(2,1)}, u32[]{:S(2)}, u32[]{:S(2)}) collective-permute-start(bf16[256,1536]{1,0:T(8,128)(2,1)} %param.3), channel_id=1, source_target_pairs={{0,7},{1,0},{2,1},{3,2},{4,3},{5,4},{6,5},{7,6},{8,15},{9,8},{10,9... | collective-permute-start | bytes 2359304 | tf_op jit(solution)/shard_map/ppermute | solution.py:29
  3.6 9.9 %collective-permute-done = bf16[256,1536]{1,0:T(8,128)(2,1)S(1)} collective-permute-done((bf16[256,1536]{1,0:T(8,128)(2,1)}, bf16[256,1536]{1,0:T(8,128)(2,1)S(1)}, u32[]{:S(2)}, u32[]{:S(2)}) %collective-permute-start) | collective-permute-done | bytes 786464 | tf_op jit(solution)/shard_map/ppermute | solution.py:24
  13.5 0.0 copy-start.3
  13.5 0.0 collective-permute-start.2
  13.5 0.0 collective-permute-done.1
  13.5 3.1 %collective-permute-start.3 = (bf16[256,1536]{1,0:T(8,128)(2,1)}, bf16[256,1536]{1,0:T(8,128)(2,1)}, u32[]{:S(2)}, u32[]{:S(2)}) collective-permute-start(bf16[256,1536]{1,0:T(8,128)(2,1)} %collective-permute-done.1), channel_id=1, source_target_pairs={{0,7},{1,0},{2,1},{3,2},{4,3},{5,4},{6,5},{7,6},{8,15},{9,8},{10,9... | collective-permute-start | bytes 2359304 | tf_op jit(solution)/shard_map/ppermute | solution.py:29
  16.6 9.7 %collective-permute-done.2 = bf16[256,1536]{1,0:T(8,128)(2,1)} collective-permute-done((bf16[256,1536]{1,0:T(8,128)(2,1)S(1)}, bf16[256,1536]{1,0:T(8,128)(2,1)}, u32[]{:S(2)}, u32[]{:S(2)}) %collective-permute-start.2) | collective-permute-done | bytes 786464 | tf_op jit(solution)/shard_map/ppermute | solution.py:24
  26.2 0.0 collective-permute-start.4
  26.2 2.6 %copy.5 = bf16[256,3072]{0,1:T(8,128)(2,1)} copy(bf16[256,3072]{1,0:T(8,128)(2,1)} %param.4) | data formatting | bytes 3145728 | tf_op args[1]
  28.8 0.0 copy-done.3
  28.8 4.2 %all-to-all-start.1 = ((bf16[256,8,384]{0,2,1:T(8,128)(2,1)}), bf16[256,8,384]{0,2,1:T(8,128)(2,1)S(1)}, u32[]{:S(2)}, u32[]{:S(2)}) async-start(bf16[256,8,384]{0,2,1:T(8,128)(2,1)} %bitcast.11), calls=%async_computation.1 | async-start | bytes 3145728 | tf_op jit(solution)/shard_map/all_to_all | solution.py:103
  33.0 0.0 copy-start.2
  33.0 0.0 copy-start.4
  33.0 0.4 broadcast_in_dim.4
  33.5 0.7 copy-done.2
  34.2 0.1 constant_dynamic-update-slice_fusion.7
  34.2 0.2 copy-done.4
  34.4 0.1 constant_dynamic-update-slice_fusion.6
  34.5 0.0 collective-permute-done.3
  34.5 3.0 %collective-permute-start.5 = (bf16[256,1536]{1,0:T(8,128)(2,1)}, bf16[256,1536]{1,0:T(8,128)(2,1)S(1)}, u32[]{:S(2)}, u32[]{:S(2)}) collective-permute-start(bf16[256,1536]{1,0:T(8,128)(2,1)} %collective-permute-done.3), channel_id=1, source_target_pairs={{0,7},{1,0},{2,1},{3,2},{4,3},{5,4},{6,5},{7,6},{8,15},{9,8},{10,9... | collective-permute-start | bytes 2359304 | tf_op jit(solution)/shard_map/ppermute | solution.py:29
  37.4 1.2 constant_dynamic-update-slice_fusion.5
  38.6 3.8 %collective-permute-done.4 = bf16[256,1536]{1,0:T(8,128)(2,1)S(1)} collective-permute-done((bf16[256,1536]{1,0:T(8,128)(2,1)}, bf16[256,1536]{1,0:T(8,128)(2,1)S(1)}, u32[]{:S(2)}, u32[]{:S(2)}) %collective-permute-start.4) | collective-permute-done | bytes 786464 | tf_op jit(solution)/shard_map/ppermute | solution.py:24
  42.4 0.0 collective-permute-start.6
  42.4 1.2 constant_dynamic-update-slice_fusion.4
  43.6 1.2 constant_dynamic-update-slice_fusion.3
  44.8 0.1 constant_dynamic-update-slice_fusion.2
  44.9 14.7 %collective-permute-done.5 = bf16[256,1536]{1,0:T(8,128)(2,1)S(1)} collective-permute-done((bf16[256,1536]{1,0:T(8,128)(2,1)}, bf16[256,1536]{1,0:T(8,128)(2,1)S(1)}, u32[]{:S(2)}, u32[]{:S(2)}) %collective-permute-start.5) | collective-permute-done | bytes 786464 | tf_op jit(solution)/shard_map/ppermute | solution.py:29
  59.5 0.1 constant_dynamic-update-slice_fusion.1
  59.6 4.8 %collective-permute-done.6 = bf16[256,1536]{1,0:T(8,128)(2,1)S(1)} collective-permute-done((bf16[256,1536]{1,0:T(8,128)(2,1)S(1)}, bf16[256,1536]{1,0:T(8,128)(2,1)S(1)}, u32[]{:S(2)}, u32[]{:S(2)}) %collective-permute-start.6) | collective-permute-done | bytes 786464 | tf_op jit(solution)/shard_map/ppermute | solution.py:24
  64.3 0.1 constant_dynamic-update-slice_fusion
  64.4 0.0 copy-start.1
  64.4 2.6 %copy-done.1 = bf16[2048,1536]{1,0:T(8,128)(2,1)} copy-done((bf16[2048,1536]{1,0:T(8,128)(2,1)}, bf16[2048,1536]{1,0:T(8,128)(2,1)S(1)}, u32[]{:S(2)}) %copy-start.1) | copy-done | bytes 6291480
  67.1 0.0 copy-done
  67.1 4.5 %convolution_convert_fusion.1 = bf16[2048,384]{1,0:T(8,128)(2,1)} fusion(bf16[2048,1536]{1,0:T(8,128)(2,1)S(1)} %constant_dynamic-update-slice_fusion, bf16[384,1536]{1,0:T(8,128)(2,1)S(1)} %copy-done), kind=kOutput, calls=%fused_computation.12 | convolution fusion | flops 2416705536 | bytes 9043968 | tf_op jit(solution)/shard_map/dot_general | solution.py:81
  71.6 0.0 all-to-all-done.1
  71.6 7.6 %all-to-all-start = ((bf16[4,512,384]{2,1,0:T(8,128)(2,1)}), bf16[4,512,384]{2,1,0:T(8,128)(2,1)}, u32[]{:S(2)}, u32[]{:S(2)}) async-start(bf16[4,512,384]{2,1,0:T(8,128)(2,1)} %bitcast.17), calls=%async_computation | async-start | bytes 3145728 | tf_op jit(solution)/shard_map/all_to_all | solution.py:47
  79.1 1.6 copy.6
  80.7 35.6 %all-to-all-done = bf16[4,512,384]{2,1,0:T(8,128)(2,1)} async-done(((bf16[4,512,384]{2,1,0:T(8,128)(2,1)}), bf16[4,512,384]{2,1,0:T(8,128)(2,1)}, u32[]{:S(2)}, u32[]{:S(2)}) %all-to-all-start) | async-done | bytes 1572896 | tf_op jit(solution)/shard_map/all_to_all | solution.py:47
  116.3 1.7 convert_reduce_fusion
  118.0 1.5 fusion.16
  119.6 0.1 broadcast_in_dim.10
  119.7 38.3 %all_to_all.48 = bf16[4,512,384]{2,1,0:T(8,128)(2,1)} all-to-all(bf16[4,512,384]{2,1,0:T(8,128)(2,1)S(1)} %broadcast_in_dim.10), channel_id=1, replica_groups=mesh['row'=8,'col'=4,'depth'=8] {'col'}, dimensions={0} | all-to-all | bytes 3145728 | tf_op jit(solution)/shard_map/all_to_all | solution.py:53
  158.0 6.5 %all-to-all-start.3 = ((bf16[8,256,384]{2,1,0:T(8,128)(2,1)}), bf16[8,256,384]{2,1,0:T(8,128)(2,1)S(1)}, u32[]{:S(2)}, u32[]{:S(2)}) async-start(bf16[8,256,384]{2,1,0:T(8,128)(2,1)} %bitcast.13), calls=%async_computation.3 | async-start | bytes 3145728 | tf_op jit(solution)/shard_map/all_to_all | solution.py:106
  164.5 7.0 %convolution_convert_fusion = bf16[384,1536]{1,0:T(8,128)(2,1)} fusion(bf16[2048,1536]{1,0:T(8,128)(2,1)} %copy-done.1, bf16[2048,384]{1,0:T(8,128)(2,1)} %bitcast.16), kind=kOutput, calls=%fused_computation.11 | convolution fusion | flops 2424373248 | bytes 9043968 | tf_op jit(solution)/shard_map/dot_general | solution.py:87
  171.5 14.6 %all-to-all-done.3 = bf16[8,256,384]{2,1,0:T(8,128)(2,1)S(1)} async-done(((bf16[8,256,384]{2,1,0:T(8,128)(2,1)}), bf16[8,256,384]{2,1,0:T(8,128)(2,1)S(1)}, u32[]{:S(2)}, u32[]{:S(2)}) %all-to-all-start.3) | async-done | bytes 1572896 | tf_op jit(solution)/shard_map/all_to_all | solution.py:106
  186.0 1.7 copy.7
  187.7 2.6 %copy.8 = bf16[256,3072]{1,0:T(8,128)(2,1)} copy(bf16[256,3072]{0,1:T(8,128)(2,1)} %bitcast.14) | data formatting | bytes 3145728
Async XLA Ops:
  0.6 66.4 %copy-start = (bf16[384,1536]{1,0:T(8,128)(2,1)S(1)}, bf16[384,1536]{1,0:T(8,128)(2,1)}, u32[]{:S(2)}) copy-start(bf16[384,1536]{1,0:T(8,128)(2,1)} %param.5) | copy-start | bytes 3538948
  0.6 12.8 %collective-permute-start = (bf16[256,1536]{1,0:T(8,128)(2,1)}, bf16[256,1536]{1,0:T(8,128)(2,1)S(1)}, u32[]{:S(2)}, u32[]{:S(2)}) collective-permute-start(bf16[256,1536]{1,0:T(8,128)(2,1)} %param.3), channel_id=1, source_target_pairs={{0,1},{1,2},{2,3},{3,4},{4,5},{5,6},{6,7},{7,0},{8,9},{9,10},{10,1... | collective-permute-start | bytes 2359304 | tf_op jit(solution)/shard_map/ppermute | solution.py:24
  0.7 12.8 %collective-permute-start.1 = (bf16[256,1536]{1,0:T(8,128)(2,1)}, bf16[256,1536]{1,0:T(8,128)(2,1)}, u32[]{:S(2)}, u32[]{:S(2)}) collective-permute-start(bf16[256,1536]{1,0:T(8,128)(2,1)} %param.3), channel_id=1, source_target_pairs={{0,7},{1,0},{2,1},{3,2},{4,3},{5,4},{6,5},{7,6},{8,15},{9,8},{10,9... | collective-permute-start | bytes 2359304 | tf_op jit(solution)/shard_map/ppermute | solution.py:29
  13.5 15.3 %copy-start.3 = (bf16[256,1536]{1,0:T(8,128)(2,1)}, bf16[256,1536]{1,0:T(8,128)(2,1)S(1)}, u32[]{:S(2)}) copy-start(bf16[256,1536]{1,0:T(8,128)(2,1)S(1)} %collective-permute-done) | copy-start | bytes 2359300
  13.5 12.7 %collective-permute-start.2 = (bf16[256,1536]{1,0:T(8,128)(2,1)S(1)}, bf16[256,1536]{1,0:T(8,128)(2,1)}, u32[]{:S(2)}, u32[]{:S(2)}) collective-permute-start(bf16[256,1536]{1,0:T(8,128)(2,1)S(1)} %collective-permute-done), channel_id=1, source_target_pairs={{0,1},{1,2},{2,3},{3,4},{4,5},{5,6},{6,7},{7,0},{8,9},{9,10},{10,1... | collective-permute-start | bytes 2359304 | tf_op jit(solution)/shard_map/ppermute | solution.py:24
  13.5 21.0 %collective-permute-start.3 = (bf16[256,1536]{1,0:T(8,128)(2,1)}, bf16[256,1536]{1,0:T(8,128)(2,1)}, u32[]{:S(2)}, u32[]{:S(2)}) collective-permute-start(bf16[256,1536]{1,0:T(8,128)(2,1)} %collective-permute-done.1), channel_id=1, source_target_pairs={{0,7},{1,0},{2,1},{3,2},{4,3},{5,4},{6,5},{7,6},{8,15},{9,8},{10,9... | collective-permute-start | bytes 2359304 | tf_op jit(solution)/shard_map/ppermute | solution.py:29
  26.2 16.2 %collective-permute-start.4 = (bf16[256,1536]{1,0:T(8,128)(2,1)}, bf16[256,1536]{1,0:T(8,128)(2,1)S(1)}, u32[]{:S(2)}, u32[]{:S(2)}) collective-permute-start(bf16[256,1536]{1,0:T(8,128)(2,1)} %collective-permute-done.2), channel_id=1, source_target_pairs={{0,1},{1,2},{2,3},{3,4},{4,5},{5,6},{6,7},{7,0},{8,9},{9,10},{10,1... | collective-permute-start | bytes 2359304 | tf_op jit(solution)/shard_map/ppermute | solution.py:24
  28.8 42.8 %all-to-all-start.1 = ((bf16[256,8,384]{0,2,1:T(8,128)(2,1)}), bf16[256,8,384]{0,2,1:T(8,128)(2,1)S(1)}, u32[]{:S(2)}, u32[]{:S(2)}) async-start(bf16[256,8,384]{0,2,1:T(8,128)(2,1)} %bitcast.11), calls=%async_computation.1 | async-start | bytes 3145728 | tf_op jit(solution)/shard_map/all_to_all | solution.py:103
  33.0 1.1 copy-start.2
  33.0 1.4 copy-start.4
  34.5 25.0 %collective-permute-start.5 = (bf16[256,1536]{1,0:T(8,128)(2,1)}, bf16[256,1536]{1,0:T(8,128)(2,1)S(1)}, u32[]{:S(2)}, u32[]{:S(2)}) collective-permute-start(bf16[256,1536]{1,0:T(8,128)(2,1)} %collective-permute-done.3), channel_id=1, source_target_pairs={{0,7},{1,0},{2,1},{3,2},{4,3},{5,4},{6,5},{7,6},{8,15},{9,8},{10,9... | collective-permute-start | bytes 2359304 | tf_op jit(solution)/shard_map/ppermute | solution.py:29
  42.4 21.9 %collective-permute-start.6 = (bf16[256,1536]{1,0:T(8,128)(2,1)S(1)}, bf16[256,1536]{1,0:T(8,128)(2,1)S(1)}, u32[]{:S(2)}, u32[]{:S(2)}) collective-permute-start(bf16[256,1536]{1,0:T(8,128)(2,1)S(1)} %collective-permute-done.4), channel_id=1, source_target_pairs={{0,1},{1,2},{2,3},{3,4},{4,5},{5,6},{6,7},{7,0},{8,9},{9,10},{10,1... | collective-permute-start | bytes 2359304 | tf_op jit(solution)/shard_map/ppermute | solution.py:24
  64.4 2.7 %copy-start.1 = (bf16[2048,1536]{1,0:T(8,128)(2,1)}, bf16[2048,1536]{1,0:T(8,128)(2,1)S(1)}, u32[]{:S(2)}) copy-start(bf16[2048,1536]{1,0:T(8,128)(2,1)S(1)} %constant_dynamic-update-slice_fusion) | copy-start | bytes 18874372
  71.6 44.7 %all-to-all-start = ((bf16[4,512,384]{2,1,0:T(8,128)(2,1)}), bf16[4,512,384]{2,1,0:T(8,128)(2,1)}, u32[]{:S(2)}, u32[]{:S(2)}) async-start(bf16[4,512,384]{2,1,0:T(8,128)(2,1)} %bitcast.17), calls=%async_computation | async-start | bytes 3145728 | tf_op jit(solution)/shard_map/all_to_all | solution.py:47
  158.0 28.1 %all-to-all-start.3 = ((bf16[8,256,384]{2,1,0:T(8,128)(2,1)}), bf16[8,256,384]{2,1,0:T(8,128)(2,1)S(1)}, u32[]{:S(2)}, u32[]{:S(2)}) async-start(bf16[8,256,384]{2,1,0:T(8,128)(2,1)} %bitcast.13), calls=%async_computation.3 | async-start | bytes 3145728 | tf_op jit(solution)/shard_map/all_to_all | solution.py:106
